TPU v7x, 32 devices: a whole 2x2x4 slice. The times are simulated.
32 devices in a mesh: batch: 8 (over z, y), space: 4 (over x, core).
Axes of the slice: x: 2, y: 2, z: 4, core: 2. Of those that a mesh axis runs over, the one named last changes fastest.
Arguments:
- features: bfloat16 [8, 48, 72, 1024], P('batch', 'space'), may hold values from -600 to 600
- depth_one: bfloat16 [3, 3, 1024], replicated, may hold values from -2 to 2
- gain_one: float32 [1024], replicated, may hold values from 0.25 to 1.75
- shift_one: float32 [1024], replicated, may hold values from -3 to 3
- point_one: bfloat16 [1024, 1536], replicated, may hold values from -0.1875 to 0.1875
- gain_two: float32 [1536], replicated, may hold values from 0.25 to 1.75
- shift_two: float32 [1536], replicated, may hold values from -3 to 3
- depth_two: bfloat16 [3, 3, 1536], replicated, may hold values from -2 to 2
- gain_three: float32 [1536], replicated, may hold values from 0.25 to 1.75
- shift_three: float32 [1536], replicated, may hold values from -3 to 3
- point_two: bfloat16 [1536, 2048], replicated, may hold values from -0.15625 to 0.15625
- gain_four: float32 [2048], replicated, may hold values from 0.25 to 1.75
- shift_four: float32 [2048], replicated, may hold values from -3 to 3
Outputs:
- exit_map: bfloat16 [8, 48, 72, 2048], P('batch', 'space')
All inputs are finite; a program needn't handle non-finite values.
Results may differ from a plain program's by a relative error of at most 0.0079.
Values may be sent and summed in bfloat16 or wider, within the bound.
A program may use at most 64 MiB of HBM per device.

v0:
```python
import jax
import jax.numpy as jnp
from jax import lax
from jax.sharding import PartitionSpec as P

RATE = 2


epsilon = 1e-05


def padded_2(cells, sides, width):
    for axis, dim in sides:
        count = lax.axis_size(axis)
        ends = count - 1
        head = lax.slice_in_dim(cells, 0, width, axis=dim)
        tail = lax.slice_in_dim(cells, cells.shape[dim] - width, cells.shape[dim], axis=dim)
        cells = jnp.concatenate(
            [
                lax.ppermute(tail, axis, [(i, (i + 1) % count) for i in range(ends)]),
                cells,
                lax.ppermute(head, axis, [((i + 1) % count, i) for i in range(ends)]),
            ],
            axis=dim,
        )
    return cells


def dilated_padded(padded, weight, span_rows, span_cols):
    summed = jnp.zeros((padded.shape[0], span_rows, span_cols, padded.shape[3]), jnp.float32)
    for tap_row in range(3):
        for tap_col in range(3):
            window = padded[
                :,
                tap_row * RATE : tap_row * RATE + span_rows,
                tap_col * RATE : tap_col * RATE + span_cols,
                :,
            ]
            summed = summed + window.astype(jnp.float32) * weight[tap_row, tap_col].astype(
                jnp.float32
            )
    return summed


def local_sums(values):
    return (jnp.sum(values, axis=(0, 1, 2)), jnp.sum(values * values, axis=(0, 1, 2)))


def scaled(values, totals, pixels, gain, offset):
    average = totals[0] / pixels
    variance = totals[1] / pixels - average * average
    factor = gain * lax.rsqrt(variance + epsilon)
    return jnp.maximum((values - average) * factor + offset, 0.0).astype(jnp.bfloat16)


def project(values, weight):
    shape = values.shape
    flat = values.reshape(shape[0] * shape[1] * shape[2], shape[3])
    result = jnp.dot(flat, weight, preferred_element_type=jnp.float32)
    return result.reshape(shape[0], shape[1], shape[2], weight.shape[1])


def per_device(
    features,
    depth_one,
    gain_one,
    shift_one,
    point_one,
    gain_two,
    shift_two,
    depth_two,
    gain_three,
    shift_three,
    point_two,
    gain_four,
    shift_four,
):
    span_rows = features.shape[1]
    span_cols = features.shape[2]
    n_batch = lax.axis_size("batch")
    n_space = lax.axis_size("space")
    all_pixels = features.shape[0] * span_rows * span_cols * n_batch * n_space
    padded = padded_2(features, (("space", 1),), RATE)
    padded = jnp.pad(padded, ((0, 0), (0, 0), (RATE, RATE), (0, 0)))
    first = dilated_padded(padded, depth_one, span_rows, span_cols)
    totals = lax.psum(local_sums(first), ("batch", "space"))
    act_one = scaled(first, totals, all_pixels, gain_one, shift_one)
    second = project(act_one, point_one)
    totals = lax.psum(local_sums(second), ("batch", "space"))
    act_two = scaled(second, totals, all_pixels, gain_two, shift_two)
    padded = padded_2(act_two, (("space", 1),), RATE)
    padded = jnp.pad(padded, ((0, 0), (0, 0), (RATE, RATE), (0, 0)))
    third = dilated_padded(padded, depth_two, span_rows, span_cols)
    totals = lax.psum(local_sums(third), ("batch", "space"))
    act_three = scaled(third, totals, all_pixels, gain_three, shift_three)
    fourth = project(act_three, point_two)
    totals = lax.psum(local_sums(fourth), ("batch", "space"))
    return scaled(fourth, totals, all_pixels, gain_four, shift_four)


def solution(mesh):
    return jax.shard_map(
        per_device,
        mesh=mesh,
        in_specs=(
            P("batch", "space", None, None),
            P(),
            P(),
            P(),
            P(),
            P(),
            P(),
            P(),
            P(),
            P(),
            P(),
            P(),
            P(),
        ),
        out_specs=P("batch", "space", None, None),
        check_vma=False,
    )
```

profile of v0, /device:TPU:0, one launch (start us, length us, event | category | flops | bytes accessed | tf_op | source)
XLA Modules:
  0.0 233.9 jit_solution(8019979569132292695)
XLA Ops:
  0.0 1.2 fusion.17
  1.3 2.5 %collective-permute-start = (bf16[1,2,72,1024]{3,2,1,0:T(8,128)(2,1)S(1)}, bf16[1,2,72,1024]{3,2,1,0:T(8,128)(2,1)S(1)}, u32[]{:S(2)}, u32[]{:S(2)}) collective-permute-start(bf16[1,2,72,1024]{3,2,1,0:T(8,128)(2,1)S(1)} %get-tuple-element.34), channel_id=1, source_target_pairs={{0,1},{1,2},{2,3},{4,5},{5,6},{6,7},{8,9},{9,10},{10,11},{12,13},{... | collective-permute-start | bytes 884744 | tf_op jit(solution)/shard_map/ppermute | solution.py:20
  3.8 1.3 collective-permute-start.1
  5.1 0.9 slice_convert_fusion.8
  6.0 3.4 %collective-permute-done.1 = bf16[1,2,72,1024]{3,2,1,0:T(8,128)(2,1)S(1)} collective-permute-done((bf16[1,2,72,1024]{3,2,1,0:T(8,128)(2,1)S(1)}, bf16[1,2,72,1024]{3,2,1,0:T(8,128)(2,1)S(1)}, u32[]{:S(2)}, u32[]{:S(2)}) %collective-permute-start.1) | collective-permute-done | bytes 294944 | tf_op jit(solution)/shard_map/ppermute | solution.py:22
  9.4 2.3 %fusion.11 = bf16[1,16,76,1024]{3,2,1,0:T(8,128)(2,1)S(1)} fusion(bf16[1,2,72,1024]{3,2,1,0:T(8,128)(2,1)S(1)} %collective-permute-done.1, bf16[1,12,72,1024]{3,2,1,0:T(8,128)(2,1)} %param.13, bf16[1,2,72,1024]{3,2,1,0:T(8,128)(2,1)S(1)} %collective-permute-done), kind=kLoop, calls=%fused_computation.27 | loop fusion | flops 14942208 | bytes 4849664 | tf_op jit(solution)/shard_map/concatenate | solution.py:18
  11.7 5.5 %fusion.15 = (f32[1024]{0:T(1024)S(1)}, f32[1024]{0:T(1024)S(1)}, f32[1,12,72,1024]{3,2,1,0:T(8,128)}) fusion(f32[1024]{0:T(1024)S(1)} %bitcast.28, bf16[1,16,76,1024]{3,2,1,0:T(8,128)(2,1)S(1)} %fusion.11, f32[1024]{0:T(1024)S(1)} %bitcast.29, bf16[1,2,72,1024]{3,2,1,0:T(8,128)(2,1)S(1)} %collective-permute-done.1, ...), kind=kLoop, calls=%fused_computation.59 | loop fusion | flops 27424768 | bytes 16560128 | tf_op jit(solution)/shard_map/reduce_sum | solution.py:46
  17.2 44.1 %all-reduce.5 = (f32[1024]{0:T(1024)S(1)}, f32[1024]{0:T(1024)S(1)}) all-reduce(f32[1024]{0:T(1024)S(1)} %get-tuple-element.12, f32[1024]{0:T(1024)S(1)} %get-tuple-element.11), channel_id=1, replica_groups=mesh['batch'=8,'space'=4] {'batch','space'}, use_global_device_ids=true, to_apply=%region_3.4 | all-reduce | flops 2048 | bytes 16384 | tf_op jit(solution)/shard_map/psum | solution.py:86
  61.4 2.6 %maximum_convert_fusion.3 = bf16[1,12,72,1024]{3,2,1,0:T(8,128)(2,1)S(1)} fusion(f32[1,12,72,1024]{3,2,1,0:T(8,128)} %get-tuple-element.31, f32[1024]{0:T(1024)S(1)} %copy-done.9, f32[1024]{0:T(1024)S(1)} %get-tuple-element.52, f32[1024]{0:T(1024)S(1)} %get-tuple-element.51), kind=kLoop, calls=%fused_computation.18 | loop fusion | flops 4423680 | bytes 5320704 | tf_op jit(solution)/shard_map/convert_element_type | solution.py:53
  64.0 4.7 %fusion.14 = (f32[1536]{0:T(1024)S(1)}, f32[1536]{0:T(1024)S(1)}, f32[864,1536]{1,0:T(8,128)}) fusion(bf16[864,1024]{1,0:T(8,128)(2,1)S(1)} %bitcast.20, bf16[1024,1536]{1,0:T(8,128)(2,1)S(1)} %copy-done), kind=kOutput, calls=%fused_computation.58 | convolution fusion | flops 2721887232 | bytes 10235904 | tf_op jit(solution)/shard_map/dot_general | solution.py:59
  68.7 40.2 %all-reduce.4 = (f32[1536]{0:T(1024)S(1)}, f32[1536]{0:T(1024)S(1)}) all-reduce(f32[1536]{0:T(1024)S(1)} %get-tuple-element.10, f32[1536]{0:T(1024)S(1)} %get-tuple-element.9), channel_id=1, replica_groups=mesh['batch'=8,'space'=4] {'batch','space'}, use_global_device_ids=true, to_apply=%region_7.8 | all-reduce | flops 3072 | bytes 24576 | tf_op jit(solution)/shard_map/psum | solution.py:89
  108.9 3.3 %maximum_convert_fusion.2 = bf16[1,12,72,1536]{3,2,1,0:T(8,128)(2,1)S(1)} fusion(f32[1,12,72,1536]{3,2,1,0:T(8,128)} %bitcast.18, f32[1536]{0:T(1024)S(1)} %copy-done.3, f32[1536]{0:T(1024)S(1)} %get-tuple-element.50, f32[1536]{0:T(1024)S(1)} %get-tuple-element.49), kind=kLoop, calls=%fused_computation.10 | loop fusion | flops 6635520 | bytes 7981056 | tf_op jit(solution)/shard_map/convert_element_type | solution.py:53
  112.3 0.1 fusion.16
  112.3 1.3 collective-permute-start.2
  113.7 1.3 collective-permute-start.3
  115.0 0.1 convert_reduce_fusion.8
  115.1 4.7 %collective-permute-done.3 = bf16[1,2,72,1536]{3,2,1,0:T(8,128)(2,1)S(1)} collective-permute-done((bf16[1,2,72,1536]{3,2,1,0:T(8,128)(2,1)S(1)}, bf16[1,2,72,1536]{3,2,1,0:T(8,128)(2,1)S(1)}, u32[]{:S(2)}, u32[]{:S(2)}) %collective-permute-start.3) | collective-permute-done | bytes 442400 | tf_op jit(solution)/shard_map/ppermute | solution.py:22
  119.8 1.7 fusion.6
  121.6 7.6 %fusion.13 = (f32[1536]{0:T(1024)S(1)}, f32[1536]{0:T(1024)S(1)}, f32[1,12,72,1536]{3,2,1,0:T(8,128)}) fusion(f32[1536]{0:T(1024)S(1)} %get-tuple-element.20, bf16[1,16,76,1536]{3,2,1,0:T(8,128)(2,1)S(1)} %fusion.6, f32[1536]{0:T(1024)S(1)} %get-tuple-element.21, bf16[1,2,72,1536]{3,2,1,0:T(8,128)(2,1)S(1)} %collective-permute-done.3, ...), kind=kLoop, calls=%fused_computation.57 | loop fusion | flops 41137152 | bytes 24840192 | tf_op jit(solution)/shard_map/reduce_sum | solution.py:46
  129.2 44.4 %all-reduce.3 = (f32[1536]{0:T(1024)S(1)}, f32[1536]{0:T(1024)S(1)}) all-reduce(f32[1536]{0:T(1024)S(1)} %get-tuple-element.8, f32[1536]{0:T(1024)S(1)} %get-tuple-element.7), channel_id=1, replica_groups=mesh['batch'=8,'space'=4] {'batch','space'}, use_global_device_ids=true, to_apply=%region_11.12 | all-reduce | flops 3072 | bytes 24576 | tf_op jit(solution)/shard_map/psum | solution.py:94
  173.6 3.3 %maximum_convert_fusion.1 = bf16[1,12,72,1536]{3,2,1,0:T(8,128)(2,1)S(1)} fusion(f32[1,12,72,1536]{3,2,1,0:T(8,128)} %get-tuple-element.30, f32[1536]{0:T(1024)S(1)} %copy-done.4, f32[1536]{0:T(1024)S(1)} %get-tuple-element.48, f32[1536]{0:T(1024)S(1)} %get-tuple-element.47), kind=kLoop, calls=%fused_computation.7 | loop fusion | flops 6635520 | bytes 7981056 | tf_op jit(solution)/shard_map/convert_element_type | solution.py:53
  177.0 10.8 %fusion.12 = (f32[2048]{0:T(1024)S(1)}, f32[2048]{0:T(1024)S(1)}, f32[864,2048]{1,0:T(8,128)}) fusion(bf16[864,1536]{1,0:T(8,128)(2,1)S(1)} %bitcast.19, bf16[1536,2048]{1,0:T(8,128)(2,1)} %param.23), kind=kOutput, calls=%fused_computation.56 | convolution fusion | flops 5441122304 | bytes 16039936 | tf_op jit(solution)/shard_map/dot_general | solution.py:59
  187.8 40.2 %all-reduce.2 = (f32[2048]{0:T(1024)S(1)}, f32[2048]{0:T(1024)S(1)}) all-reduce(f32[2048]{0:T(1024)S(1)} %get-tuple-element.6, f32[2048]{0:T(1024)S(1)} %get-tuple-element.5), channel_id=1, replica_groups=mesh['batch'=8,'space'=4] {'batch','space'}, use_global_device_ids=true, to_apply=%region_15.16 | all-reduce | flops 4096 | bytes 32768 | tf_op jit(solution)/shard_map/psum | solution.py:97
  228.0 6.0 %maximum_convert_fusion = bf16[1,12,72,2048]{3,2,1,0:T(8,128)(2,1)} fusion(f32[1,12,72,2048]{3,2,1,0:T(8,128)} %bitcast.17, f32[2048]{0:T(1024)S(1)} %copy-done.5, f32[2048]{0:T(1024)S(1)} %get-tuple-element.46, f32[2048]{0:T(1024)S(1)} %get-tuple-element.45), kind=kLoop, calls=%fused_computation.5 | loop fusion | flops 8847360 | bytes 10641408 | tf_op jit(solution)/shard_map/convert_element_type | solution.py:53
  (28 shorter events, 0.1 us)
Async XLA Ops:
  0.0 64.0 %copy-start = (bf16[1024,1536]{1,0:T(8,128)(2,1)S(1)}, bf16[1024,1536]{1,0:T(8,128)(2,1)}, u32[]{:S(2)}) copy-start(bf16[1024,1536]{1,0:T(8,128)(2,1)} %param.17) | copy-start | bytes 9437188
  0.0 11.7 %copy-start.1 = (bf16[1,12,72,1024]{3,2,1,0:T(8,128)(2,1)S(1)}, bf16[1,12,72,1024]{3,2,1,0:T(8,128)(2,1)}, u32[]{:S(2)}) copy-start(bf16[1,12,72,1024]{3,2,1,0:T(8,128)(2,1)} %param.13) | copy-start | bytes 5308420
  1.3 4.7 %collective-permute-start = (bf16[1,2,72,1024]{3,2,1,0:T(8,128)(2,1)S(1)}, bf16[1,2,72,1024]{3,2,1,0:T(8,128)(2,1)S(1)}, u32[]{:S(2)}, u32[]{:S(2)}) collective-permute-start(bf16[1,2,72,1024]{3,2,1,0:T(8,128)(2,1)S(1)} %get-tuple-element.34), channel_id=1, source_target_pairs={{0,1},{1,2},{2,3},{4,5},{5,6},{6,7},{8,9},{9,10},{10,11},{12,13},{... | collective-permute-start | bytes 884744 | tf_op jit(solution)/shard_map/ppermute | solution.py:20
  3.8 5.6 %collective-permute-start.1 = (bf16[1,2,72,1024]{3,2,1,0:T(8,128)(2,1)S(1)}, bf16[1,2,72,1024]{3,2,1,0:T(8,128)(2,1)S(1)}, u32[]{:S(2)}, u32[]{:S(2)}) collective-permute-start(bf16[1,2,72,1024]{3,2,1,0:T(8,128)(2,1)S(1)} %get-tuple-element.35), channel_id=1, source_target_pairs={{1,0},{2,1},{3,2},{5,4},{6,5},{7,6},{9,8},{10,9},{11,10},{13,12},{... | collective-permute-start | bytes 884744 | tf_op jit(solution)/shard_map/ppermute | solution.py:22
  11.7 49.6 %copy-start.10 = (f32[1024]{0:T(1024)S(1)}, f32[1024]{0:T(1024)}, u32[]{:S(2)}) copy-start(f32[1024]{0:T(1024)} %param.15) | copy-start | bytes 12292
  11.7 49.6 %copy-start.9 = (f32[1024]{0:T(1024)S(1)}, f32[1024]{0:T(1024)}, u32[]{:S(2)}) copy-start(f32[1024]{0:T(1024)} %param.16) | copy-start | bytes 12292
  64.0 45.0 %copy-start.6 = (f32[1536]{0:T(1024)S(1)}, f32[1536]{0:T(1024)}, u32[]{:S(2)}) copy-start(f32[1536]{0:T(1024)} %param.18) | copy-start | bytes 18436
  64.0 45.0 %copy-start.3 = (f32[1536]{0:T(1024)S(1)}, f32[1536]{0:T(1024)}, u32[]{:S(2)}) copy-start(f32[1536]{0:T(1024)} %param.19) | copy-start | bytes 18436
  108.9 6.0 %copy-start.2 = (bf16[3,3,1536]{2,1,0:T(4,128)(2,1)S(1)}, bf16[3,3,1536]{2,1,0:T(4,128)(2,1)}, u32[]{:S(2)}) copy-start(bf16[3,3,1536]{2,1,0:T(4,128)(2,1)} %param.20) | copy-start | bytes 82948
  112.3 2.8 %collective-permute-start.2 = (bf16[1,2,72,1536]{3,2,1,0:T(8,128)(2,1)S(1)}, bf16[1,2,72,1536]{3,2,1,0:T(8,128)(2,1)S(1)}, u32[]{:S(2)}, u32[]{:S(2)}) collective-permute-start(bf16[1,2,72,1536]{3,2,1,0:T(8,128)(2,1)S(1)} %get-tuple-element.32), channel_id=1, source_target_pairs={{0,1},{1,2},{2,3},{4,5},{5,6},{6,7},{8,9},{9,10},{10,11},{12,13},{... | collective-permute-start | bytes 1327112 | tf_op jit(solution)/shard_map/ppermute | solution.py:20
  113.7 6.2 %collective-permute-start.3 = (bf16[1,2,72,1536]{3,2,1,0:T(8,128)(2,1)S(1)}, bf16[1,2,72,1536]{3,2,1,0:T(8,128)(2,1)S(1)}, u32[]{:S(2)}, u32[]{:S(2)}) collective-permute-start(bf16[1,2,72,1536]{3,2,1,0:T(8,128)(2,1)S(1)} %get-tuple-element.33), channel_id=1, source_target_pairs={{1,0},{2,1},{3,2},{5,4},{6,5},{7,6},{9,8},{10,9},{11,10},{13,12},{... | collective-permute-start | bytes 1327112 | tf_op jit(solution)/shard_map/ppermute | solution.py:22
  121.6 52.1 %copy-start.7 = (f32[1536]{0:T(1024)S(1)}, f32[1536]{0:T(1024)}, u32[]{:S(2)}) copy-start(f32[1536]{0:T(1024)} %param.21) | copy-start | bytes 18436
  121.6 52.1 %copy-start.4 = (f32[1536]{0:T(1024)S(1)}, f32[1536]{0:T(1024)}, u32[]{:S(2)}) copy-start(f32[1536]{0:T(1024)} %param.22) | copy-start | bytes 18436
  177.0 51.0 %copy-start.8 = (f32[2048]{0:T(1024)S(1)}, f32[2048]{0:T(1024)}, u32[]{:S(2)}) copy-start(f32[2048]{0:T(1024)} %param.24) | copy-start | bytes 24580
  177.0 51.0 %copy-start.5 = (f32[2048]{0:T(1024)S(1)}, f32[2048]{0:T(1024)}, u32[]{:S(2)}) copy-start(f32[2048]{0:T(1024)} %param.25) | copy-start | bytes 24580
where the time goes:
time: 235 us; the launch traced here: 234 us
  blocking collectives  169 us (72%)
  other arithmetic  33.4 us (14%)
  matrix products  15.5 us (7%)
  waiting for transfers between devices  8.05 us (3%)
  starting transfers between devices  6.45 us (3%)
    psum x1, blocking collectives, per_device(): totals = lax.psum(local_sums(third), ('batch', 'space'))  44.4 us
    psum x1, blocking collectives, per_device(): totals = lax.psum(local_sums(first), ('batch', 'space'))  44.1 us
    psum x1, blocking collectives, per_device(): totals = lax.psum(local_sums(second), ('batch', 'space'))  40.2 us
    psum x1, blocking collectives, per_device(): totals = lax.psum(local_sums(fourth), ('batch', 'space'))  40.2 us
    dot_general x2, matrix products, project(): result = jnp.dot(flat, weight, preferred_element_type=jnp.float32)  15.5 us
    convert_element_type x4, other arithmetic, scaled(): jnp.maximum((values - average) * factor + offset, 0.0).astype(jnp.bfloat16)  15.2 us
    reduce_sum x2, other arithmetic, local_sums(): jnp.sum(values, axis=(0, 1, 2))  13.1 us
    ppermute x2, waiting for transfers between devices, padded_2(): lax.ppermute(head, axis, [((i + 1) % count, i) for i in range(ends)])  8.05 us
  transfers between devices with their start and end apart: 4, of which 2 were waited for; matrix products, arithmetic and copies ran while one was open for 0% of the time, Pallas kernels for 0%

commit v1 on v0

v1 whole, which is shorter than its diff:
```python
import functools

import jax
import jax.numpy as jnp
from jax import lax
from jax.experimental import pallas as pl
from jax.experimental.pallas import tpu as pltpu
from jax.sharding import PartitionSpec as P

RATE = 2
PIECES = 4
EPS = 1e-05
LANES = 128
PAD = 8
NCOL = 256
MESH = pl.DeviceIdType.MESH
F32 = jnp.float32
BF16 = jnp.bfloat16


def block_rows(pixels):
    for rows in (144, 96, 48, 32, 16):
        if pixels % rows == 0:
            return rows
    return pixels


def kernel(
    n_space,
    n_batch,
    x_hbm,
    w1_hbm,
    w2_hbm,
    d1_ref,
    d2_ref,
    g1_ref,
    b1_ref,
    g2_ref,
    b2_ref,
    g3_ref,
    b3_ref,
    g4_ref,
    b4_ref,
    fourth,
    mean_out,
    fac_out,
    shift_out,
    x_ref,
    w1_ref,
    w2_ref,
    halo1,
    edge2,
    halo2,
    xp,
    first,
    act1,
    second,
    act3,
    par_ref,
    sa0,
    sa1,
    sa2,
    sa3,
    sb0,
    sb1,
    sb2,
    sb3,
    coef,
    load_sem,
    h1_send,
    h1_recv,
    h2_send,
    h2_recv,
    a_send,
    a_recv,
    b_send,
    b_recv,
):
    rows, cols, c_in = x_hbm.shape
    c_mid = w1_hbm.shape[1]
    c_out = w2_hbm.shape[1]
    pixels = rows * cols
    edge = RATE * cols
    total = float(pixels * n_space * n_batch)
    step = block_rows(pixels)
    n_in, n_mid, n_out = c_in // LANES, c_mid // LANES, c_out // LANES
    sp = lax.axis_index("space")
    bt = lax.axis_index("batch")
    has_top = sp > 0
    has_bot = sp < n_space - 1
    sa = (sa0, sa1, sa2, sa3)
    sb = (sb0, sb1, sb2, sb3)

    load_x = pltpu.make_async_copy(x_hbm, x_ref, load_sem.at[0])
    load_w1 = pltpu.make_async_copy(w1_hbm, w1_ref, load_sem.at[1])
    load_w2 = pltpu.make_async_copy(w2_hbm, w2_ref, load_sem.at[2])

    barrier = pltpu.get_barrier_semaphore()
    for d in range(1, n_space):
        pl.semaphore_signal(
            barrier, inc=1, device_id={"space": lax.rem(sp + d, n_space)}, device_id_type=MESH
        )
    for d in range(1, n_batch):
        pl.semaphore_signal(
            barrier, inc=1, device_id={"batch": lax.rem(bt + d, n_batch)}, device_id_type=MESH
        )
    load_x.start()
    load_w1.start()
    load_w2.start()

    def clear(j, carry):
        for r in range(rows + 2 * RATE):
            xp[j, r, 0:PAD, :] = jnp.zeros((PAD, LANES), F32)
            xp[j, r, PAD + cols : PAD + cols + PAD, :] = jnp.zeros((PAD, LANES), F32)
        return carry

    lax.fori_loop(0, c_mid // LANES, clear, 0)
    at = 0
    for ref in (g1_ref, b1_ref, g2_ref, b2_ref, g3_ref, b3_ref, g4_ref, b4_ref):
        for j in range(ref.shape[0] // LANES):
            par_ref[at : at + 1, :] = ref[j * LANES : (j + 1) * LANES].reshape(1, LANES)
            at += 1
    load_x.wait()
    pl.semaphore_wait(barrier, n_space - 1 + n_batch - 1)

    wide_in = c_in // PIECES

    def up1(p):
        lanes = pl.ds(p * wide_in, wide_in)
        return pltpu.make_async_remote_copy(
            src_ref=x_ref.at[pl.ds(rows - RATE, RATE), :, lanes],
            dst_ref=halo1.at[0, :, :, lanes],
            send_sem=h1_send.at[0, p],
            recv_sem=h1_recv.at[0, p],
            device_id={"space": sp + 1},
            device_id_type=MESH,
        )

    def down1(p):
        lanes = pl.ds(p * wide_in, wide_in)
        return pltpu.make_async_remote_copy(
            src_ref=x_ref.at[pl.ds(0, RATE), :, lanes],
            dst_ref=halo1.at[1, :, :, lanes],
            send_sem=h1_send.at[1, p],
            recv_sem=h1_recv.at[1, p],
            device_id={"space": sp - 1},
            device_id_type=MESH,
        )

    for p in range(PIECES):

        @pl.when(has_bot)
        def _():
            up1(p).start()

        @pl.when(has_top)
        def _():
            down1(p).start()

    @pl.when(jnp.logical_not(has_top))
    def _():
        halo1[0] = jnp.zeros(halo1.shape[1:], BF16)

    @pl.when(jnp.logical_not(has_bot))
    def _():
        halo1[1] = jnp.zeros(halo1.shape[1:], BF16)

    def taps(d_ref, lanes):
        return [
            [d_ref[a, b : b + 1, lanes].astype(F32) for b in range(3)] for a in range(3)
        ]

    def conv_row(j, r, filt):
        acc = None
        for a in range(3):
            for b in range(3):
                term = xp[j, r + RATE * a, pl.ds(PAD + RATE * (b - 1), cols), :] * filt[a][b]
                acc = term if acc is None else acc + term
        return acc

    def lanes_of(j):
        return pl.ds(pl.multiple_of(j * LANES, LANES), LANES)

    def fold(v):
        s = v[0:8]
        for k in range(1, v.shape[0] // 8):
            s = s + v[8 * k : 8 * k + 8]
        return s

    def conv_rows(j, row_list, d_ref, dst, s1, s2):
        lanes = lanes_of(j)
        filt = taps(d_ref, lanes)
        for r in row_list:
            y = conv_row(j, r, filt)
            dst[r * cols : (r + 1) * cols, lanes] = y
            s1 = s1 + fold(y)
            s2 = s2 + fold(y * y)
        return s1, s2

    def put_stats(buf, slot, row, count, s1, s2):
        buf[slot, pl.ds(row, 1), :] = jnp.sum(s1, axis=0, keepdims=True)
        buf[slot, pl.ds(row + count, 1), :] = jnp.sum(s2, axis=0, keepdims=True)

    def exchange_a(i, d):
        return pltpu.make_async_remote_copy(
            src_ref=sa[i].at[sp],
            dst_ref=sa[i].at[sp],
            send_sem=a_send.at[i, d - 1],
            recv_sem=a_recv.at[i, d - 1],
            device_id={"space": lax.rem(sp + d, n_space)},
            device_id_type=MESH,
        )

    def exchange_b(i, d):
        return pltpu.make_async_remote_copy(
            src_ref=sb[i].at[bt],
            dst_ref=sb[i].at[bt],
            send_sem=b_send.at[i, d - 1],
            recv_sem=b_recv.at[i, d - 1],
            device_id={"batch": lax.rem(bt + d, n_batch)},
            device_id_type=MESH,
        )

    def reduce_stats(i, count, at, between=lambda: None):
        for d in range(1, n_space):
            exchange_a(i, d).start()
        between()
        for d in range(1, n_space):
            exchange_a(i, d).wait_recv()
        s = sa[i][0]
        for k in range(1, n_space):
            s = s + sa[i][k]
        sb[i][bt] = s
        for d in range(1, n_batch):
            exchange_b(i, d).start()
        for d in range(1, n_batch):
            exchange_b(i, d).wait_recv()
        s = sb[i][0]
        for k in range(1, n_batch):
            s = s + sb[i][k]
        mean = s[:count] / total
        var = s[count:] / total - mean * mean
        fac = par_ref[at : at + count] * lax.rsqrt(var + EPS)
        coef[0, 0:count] = mean
        coef[1, 0:count] = fac
        coef[2, 0:count] = par_ref[at + count : at + 2 * count]
        for d in range(1, n_space):
            exchange_a(i, d).wait_send()
        for d in range(1, n_batch):
            exchange_b(i, d).wait_send()

    def normal(v, j):
        return jnp.maximum(
            (v - coef[0, pl.ds(j, 1), :]) * coef[1, pl.ds(j, 1), :] + coef[2, pl.ds(j, 1), :], 0.0
        ).astype(BF16)

    zero8 = jnp.zeros((8, LANES), F32)
    inner = list(range(RATE, rows - RATE))
    outer = list(range(RATE)) + list(range(rows - RATE, rows))


    def conv1_inner(j, carry):
        lanes = lanes_of(j)
        for r in range(rows):
            xp[j, r + RATE, PAD : PAD + cols, :] = x_ref[r, :, lanes].astype(F32)
        s1, s2 = conv_rows(j, inner, d1_ref, first, zero8, zero8)
        coef[3, pl.ds(pl.multiple_of(j * 8, 8), 8), :] = s1
        coef[4, pl.ds(pl.multiple_of(j * 8, 8), 8), :] = s2
        return carry

    lax.fori_loop(0, n_in, conv1_inner, 0)

    def conv1_outer(j, carry):
        lanes = lanes_of(j)
        for r in range(RATE):
            xp[j, r, PAD : PAD + cols, :] = halo1[0, r, :, lanes].astype(F32)
            xp[j, rows + RATE + r, PAD : PAD + cols, :] = halo1[1, r, :, lanes].astype(F32)
        s1 = coef[3, pl.ds(pl.multiple_of(j * 8, 8), 8), :]
        s2 = coef[4, pl.ds(pl.multiple_of(j * 8, 8), 8), :]
        s1, s2 = conv_rows(j, outer, d1_ref, first, s1, s2)
        put_stats(sa0, sp, j, n_in, s1, s2)
        return carry

    for p in range(PIECES):

        @pl.when(has_top)
        def _():
            up1(p).wait_recv()

        @pl.when(has_bot)
        def _():
            down1(p).wait_recv()

        lax.fori_loop(p * n_in // PIECES, (p + 1) * n_in // PIECES, conv1_outer, 0)
    reduce_stats(0, n_in, 0)

    for p in range(PIECES):

        @pl.when(has_bot)
        def _():
            up1(p).wait_send()

        @pl.when(has_top)
        def _():
            down1(p).wait_send()

    def norm_to(src, dst, count):
        def body(j, carry):
            lanes = lanes_of(j)
            for k in range(pixels // step):
                span = slice(k * step, (k + 1) * step)
                dst[span, lanes] = normal(src[span, lanes], j)
            return carry

        lax.fori_loop(0, count, body, 0)

    norm_to(first, act1, n_in)

    def up2(n):
        return pltpu.make_async_remote_copy(
            src_ref=edge2.at[0, n],
            dst_ref=halo2.at[0, n],
            send_sem=h2_send.at[0, n],
            recv_sem=h2_recv.at[0, n],
            device_id={"space": sp + 1},
            device_id_type=MESH,
        )

    def down2(n):
        return pltpu.make_async_remote_copy(
            src_ref=edge2.at[1, n],
            dst_ref=halo2.at[1, n],
            send_sem=h2_send.at[1, n],
            recv_sem=h2_recv.at[1, n],
            device_id={"space": sp - 1},
            device_id_type=MESH,
        )

    def project(act, w_ref, dst, buf, count, after):
        def body(n, carry):
            wide = pl.ds(pl.multiple_of(n * NCOL, NCOL), NCOL)
            y = jnp.dot(act[...], w_ref[:, wide], preferred_element_type=F32)
            dst[:, wide] = y
            s1 = fold(y)
            s2 = fold(y * y)
            for q in range(NCOL // LANES):
                part = slice(q * LANES, (q + 1) * LANES)
                put_stats(buf, sp, n * (NCOL // LANES) + q, count, s1[:, part], s2[:, part])
            after(n, y)
            return carry

        lax.fori_loop(0, count * LANES // NCOL, body, 0)

    n_wide = c_mid // NCOL
    early = n_wide // 2

    def send_edges(n, y):
        edge2[0, n] = y[pixels - edge :].astype(BF16)
        edge2[1, n] = y[:edge].astype(BF16)

        @pl.when(jnp.logical_and(has_bot, n < early))
        def _():
            up2(n).start()

        @pl.when(jnp.logical_and(has_top, n < early))
        def _():
            down2(n).start()

    def send_late():
        def body(n, carry):
            @pl.when(has_bot)
            def _():
                up2(n).start()

            @pl.when(has_top)
            def _():
                down2(n).start()

            return carry

        lax.fori_loop(early, n_wide, body, 0)

    load_w1.wait()
    project(act1, w1_ref, second, sa1, n_mid, send_edges)
    reduce_stats(1, n_mid, 2 * n_in, send_late)

    def wait_edges(n, carry):
        @pl.when(has_top)
        def _():
            up2(n).wait_recv()

        @pl.when(has_bot)
        def _():
            down2(n).wait_recv()

        return carry

    @pl.when(jnp.logical_not(has_top))
    def _():
        halo2[0] = jnp.zeros(halo2.shape[1:], BF16)

    @pl.when(jnp.logical_not(has_bot))
    def _():
        halo2[1] = jnp.zeros(halo2.shape[1:], BF16)

    lax.fori_loop(0, n_wide, wait_edges, 0)

    def conv2(n, carry):
        for q in range(NCOL // LANES):
            j = n * (NCOL // LANES) + q
            lanes = lanes_of(j)
            part = slice(q * LANES, (q + 1) * LANES)
            for r in range(rows):
                v = normal(second[r * cols : (r + 1) * cols, lanes], j)
                xp[j, r + RATE, PAD : PAD + cols, :] = v.astype(F32)
            top = normal(halo2[0, n, :, part].astype(F32), j).astype(F32)
            top = jnp.where(has_top, top, 0.0)
            bot = normal(halo2[1, n, :, part].astype(F32), j).astype(F32)
            bot = jnp.where(has_bot, bot, 0.0)
            for r in range(RATE):
                xp[j, r, PAD : PAD + cols, :] = top[r * cols : (r + 1) * cols]
                xp[j, rows + RATE + r, PAD : PAD + cols, :] = bot[r * cols : (r + 1) * cols]
            s1, s2 = conv_rows(j, list(range(rows)), d2_ref, second, zero8, zero8)
            put_stats(sa2, sp, j, n_mid, s1, s2)
        return carry

    lax.fori_loop(0, n_wide, conv2, 0)
    reduce_stats(2, n_mid, 2 * n_in + 2 * n_mid)
    norm_to(second, act3, n_mid)

    load_w2.wait()
    project(act3, w2_ref, fourth, sa3, n_out, lambda n, y: None)
    reduce_stats(3, n_out, 2 * n_in + 4 * n_mid)

    for q, ref in enumerate((mean_out, fac_out, shift_out)):
        for j in range(n_out):
            ref[0:1, j * LANES : (j + 1) * LANES] = coef[q, j : j + 1, :]

    def drain(n, carry):
        @pl.when(has_bot)
        def _():
            up2(n).wait_send()

        @pl.when(has_top)
        def _():
            down2(n).wait_send()

        return carry

    lax.fori_loop(0, n_wide, drain, 0)


def per_device(
    features,
    depth_one,
    gain_one,
    shift_one,
    point_one,
    gain_two,
    shift_two,
    depth_two,
    gain_three,
    shift_three,
    point_two,
    gain_four,
    shift_four,
):
    samples, span_rows, cols, c_in = features.shape
    rows = samples * span_rows
    assert samples == 1
    c_mid = point_one.shape[1]
    c_out = point_two.shape[1]
    pixels = rows * cols
    n_space = lax.axis_size("space")
    n_batch = lax.axis_size("batch")
    n_in, n_mid, n_out = c_in // LANES, c_mid // LANES, c_out // LANES
    any_spec = pl.BlockSpec(memory_space=pl.ANY)
    vmem = pl.BlockSpec(memory_space=pltpu.VMEM)
    counts = (n_in, n_mid, n_mid, n_out)
    edge = RATE * cols
    n_wide = c_mid // NCOL
    coef_rows = max(n_out, 8 * n_in)
    DMA = pltpu.SemaphoreType.DMA
    fourth, mean, fac, shift = pl.pallas_call(
        functools.partial(kernel, n_space, n_batch),
        out_shape=(
            pltpu.VMEM((pixels, c_out), F32),
            jax.ShapeDtypeStruct((1, c_out), F32),
            jax.ShapeDtypeStruct((1, c_out), F32),
            jax.ShapeDtypeStruct((1, c_out), F32),
        ),
        in_specs=[any_spec] * 3 + [vmem] * 10,
        out_specs=(vmem,) * 4,
        scratch_shapes=[
            pltpu.VMEM((rows, cols, c_in), BF16),
            pltpu.VMEM((c_in, c_mid), BF16),
            pltpu.VMEM((c_mid, c_out), BF16),
            pltpu.VMEM((2, RATE, cols, c_in), BF16),
            pltpu.VMEM((2, n_wide, edge, NCOL), BF16),
            pltpu.VMEM((2, n_wide, edge, NCOL), BF16),
            pltpu.VMEM((n_mid, rows + 2 * RATE, cols + 2 * PAD, LANES), F32),
            pltpu.VMEM((pixels, c_in), F32),
            pltpu.VMEM((pixels, c_in), BF16),
            pltpu.VMEM((pixels, c_mid), F32),
            pltpu.VMEM((pixels, c_mid), BF16),
            pltpu.VMEM((2 * sum((n_in, n_mid, n_mid, n_out)), LANES), F32),
        ]
        + [pltpu.VMEM((n_space, 2 * c, LANES), F32) for c in counts]
        + [pltpu.VMEM((n_batch, 2 * c, LANES), F32) for c in counts]
        + [
            pltpu.VMEM((5, coef_rows, LANES), F32),
            DMA((3,)),
            DMA((2, PIECES)),
            DMA((2, PIECES)),
            DMA((2, n_wide)),
            DMA((2, n_wide)),
            DMA((4, n_space - 1)),
            DMA((4, n_space - 1)),
            DMA((4, n_batch - 1)),
            DMA((4, n_batch - 1)),
        ],
        compiler_params=pltpu.CompilerParams(
            collective_id=0, has_side_effects=True, vmem_limit_bytes=56 * 1024 * 1024
        ),
        name="exit_block",
    )(
        features.reshape(rows, cols, c_in),
        point_one,
        point_two,
        depth_one,
        depth_two,
        *(
            v
            for v in (
                gain_one,
                shift_one,
                gain_two,
                shift_two,
                gain_three,
                shift_three,
                gain_four,
                shift_four,
            )
        ),
    )
    out = jnp.maximum((fourth - mean) * fac + shift, 0.0).astype(BF16)
    return out.reshape(samples, span_rows, cols, c_out)


def solution(mesh):
    return jax.shard_map(
        per_device,
        mesh=mesh,
        in_specs=(P("batch", "space", None, None),) + (P(),) * 12,
        out_specs=P("batch", "space", None, None),
        check_vma=False,
    )
```

time: 235 us -> 64.9 us (0.28)
  blocking collectives: 169 us -> 0 us
  Pallas kernels: 0 us -> 60.9 us
  other arithmetic: 33.4 us -> 3.68 us
  matrix products: 15.5 us -> 0 us
  waiting for transfers between devices: 8.05 us -> 0 us
  starting transfers between devices: 6.45 us -> 0 us
    psum x4 -> x0, blocking collectives: 169 us -> none  [the longest x1 44.4 us: per_device(): totals = lax.psum(local_sums(third), ('batch', 'space'))]
    pallas_call x0 -> x1, Pallas kernels: none -> 60.9 us  [per_device(): pl.pallas_call(functools.partial(kernel, n_space, n_batch), out_shape=(pl...]
    dot_general x2 -> x0, matrix products: 15.5 us -> none  [project(): result = jnp.dot(flat, weight, preferred_element_type=jnp.float32)]
    reduce_sum x2 -> x0, other arithmetic: 13.1 us -> none  [local_sums(): jnp.sum(values, axis=(0, 1, 2))]
    convert_element_type x6 -> x1, other arithmetic: 16.2 us -> 3.68 us  [per_device(): out = jnp.maximum((fourth - mean) * fac + shift, 0.0).astype(BF16)]
    ppermute x4 -> x0, waiting for transfers between devices: 8.05 us -> none  [the longest x2 8.05 us: padded_2(): lax.ppermute(head, axis, [((i + 1) % count, i) for i in range(ends)])]
    ppermute x4 -> x0, starting transfers between devices: 6.45 us -> none  [the longest x2 3.86 us: padded_2(): lax.ppermute(tail, axis, [(i, (i + 1) % count) for i in range(ends)])]
    concatenate x2 -> x0, other arithmetic: 4.05 us -> none  [padded_2(): jnp.concatenate([lax.ppermute(tail, axis, [(i, (i + 1) % count) for i in...]
  transfers between devices with their start and end apart: 4 -> 0, of which waited for: 2 -> 0; matrix products, arithmetic and copies ran while one was open for 0% -> 0% of each run, Pallas kernels for 0% -> 0%
where the time goes in v1:
time: 64.9 us; the launch traced here: 64.6 us
  Pallas kernels  60.9 us (94%)
  other arithmetic  3.68 us (6%)
    pallas_call x1, Pallas kernels, per_device(): pl.pallas_call(functools.partial(kernel, n_space, n_batch), out_shape=(pl...  60.9 us
    convert_element_type x1, other arithmetic, per_device(): out = jnp.maximum((fourth - mean) * fac + shift, 0.0).astype(BF16)  3.68 us

profile of v1, /device:TPU:0, one launch (start us, length us, event | category | flops | bytes accessed | tf_op | source)
XLA Modules:
  0.0 64.6 jit_solution(11113380833858542177)
XLA Ops:
  0.0 60.9 %exit_block.1 = (f32[864,2048]{1,0:T(8,128)S(1)}, f32[1,2048]{1,0:T(1,128)}, f32[1,2048]{1,0:T(1,128)}, f32[1,2048]{1,0:T(1,128)}) custom-call(bf16[12,72,1024]{2,1,0:T(8,128)(2,1)} %bitcast.5, bf16[1024,1536]{1,0:T(8,128)(2,1)} %w1_hbm.1, bf16[1536,2048]{1,0:T(8,128)(2,1)} %w2_hbm.1, bf16[3,3,1024]{2,1,0:T(4,128)(2,1)} %d1_ref.1, ...), custom_call_target="tpu_custom_call" | custom-call | tf_op jit(solution)/shard_map/exit_block/pallas_call | solution.py:484
  60.9 3.7 %maximum_convert_fusion = bf16[864,2048]{1,0:T(8,128)(2,1)} fusion(f32[864,2048]{1,0:T(8,128)S(1)} %get-tuple-element.9, f32[2048]{0:T(1024)} %bitcast.8, f32[2048]{0:T(1024)} %bitcast.7, f32[2048]{0:T(1024)} %bitcast.6), kind=kLoop, calls=%fused_computation | loop fusion | flops 8847360 | bytes 10641408 | tf_op jit(solution)/shard_map/convert_element_type | solution.py:546

commit v2 on v1

--- a/solution.py
+++ b/solution.py
@@ -61,10 +61,16 @@
     sa1,
     sa2,
     sa3,
+    sa4,
+    sa5,
+    sa6,
     sb0,
     sb1,
     sb2,
     sb3,
+    sb4,
+    sb5,
+    sb6,
     coef,
     load_sem,
     h1_send,
@@ -88,8 +94,8 @@
     bt = lax.axis_index("batch")
     has_top = sp > 0
     has_bot = sp < n_space - 1
-    sa = (sa0, sa1, sa2, sa3)
-    sb = (sb0, sb1, sb2, sb3)
+    sa = (sa0, sa1, sa2, sa3, sa4, sa5, sa6)
+    sb = (sb0, sb1, sb2, sb3, sb4, sb5, sb6)
 
     load_x = pltpu.make_async_copy(x_hbm, x_ref, load_sem.at[0])
     load_w1 = pltpu.make_async_copy(w1_hbm, w1_ref, load_sem.at[1])
@@ -221,10 +227,11 @@
             device_id_type=MESH,
         )
 
-    def reduce_stats(i, count, at, between=lambda: None):
+    def start(i):
         for d in range(1, n_space):
             exchange_a(i, d).start()
-        between()
+
+    def relay(i):
         for d in range(1, n_space):
             exchange_a(i, d).wait_recv()
         s = sa[i][0]
@@ -233,6 +240,8 @@
         sb[i][bt] = s
         for d in range(1, n_batch):
             exchange_b(i, d).start()
+
+    def finish(i, j0, count, at, full):
         for d in range(1, n_batch):
             exchange_b(i, d).wait_recv()
         s = sb[i][0]
@@ -240,10 +249,10 @@
             s = s + sb[i][k]
         mean = s[:count] / total
         var = s[count:] / total - mean * mean
-        fac = par_ref[at : at + count] * lax.rsqrt(var + EPS)
-        coef[0, 0:count] = mean
-        coef[1, 0:count] = fac
-        coef[2, 0:count] = par_ref[at + count : at + 2 * count]
+        fac = par_ref[at + j0 : at + j0 + count] * lax.rsqrt(var + EPS)
+        coef[0, j0 : j0 + count] = mean
+        coef[1, j0 : j0 + count] = fac
+        coef[2, j0 : j0 + count] = par_ref[at + full + j0 : at + full + j0 + count]
         for d in range(1, n_space):
             exchange_a(i, d).wait_send()
         for d in range(1, n_batch):
@@ -270,16 +279,21 @@
 
     lax.fori_loop(0, n_in, conv1_inner, 0)
 
-    def conv1_outer(j, carry):
-        lanes = lanes_of(j)
-        for r in range(RATE):
-            xp[j, r, PAD : PAD + cols, :] = halo1[0, r, :, lanes].astype(F32)
-            xp[j, rows + RATE + r, PAD : PAD + cols, :] = halo1[1, r, :, lanes].astype(F32)
-        s1 = coef[3, pl.ds(pl.multiple_of(j * 8, 8), 8), :]
-        s2 = coef[4, pl.ds(pl.multiple_of(j * 8, 8), 8), :]
-        s1, s2 = conv_rows(j, outer, d1_ref, first, s1, s2)
-        put_stats(sa0, sp, j, n_in, s1, s2)
-        return carry
+    half_in = n_in // 2
+
+    def conv1_outer(buf, j0):
+        def body(j, carry):
+            lanes = lanes_of(j)
+            for r in range(RATE):
+                xp[j, r, PAD : PAD + cols, :] = halo1[0, r, :, lanes].astype(F32)
+                xp[j, rows + RATE + r, PAD : PAD + cols, :] = halo1[1, r, :, lanes].astype(F32)
+            s1 = coef[3, pl.ds(pl.multiple_of(j * 8, 8), 8), :]
+            s2 = coef[4, pl.ds(pl.multiple_of(j * 8, 8), 8), :]
+            s1, s2 = conv_rows(j, outer, d1_ref, first, s1, s2)
+            put_stats(buf, sp, j - j0, half_in, s1, s2)
+            return carry
+
+        return body
 
     for p in range(PIECES):
 
@@ -291,8 +305,15 @@
         def _():
             down1(p).wait_recv()
 
-        lax.fori_loop(p * n_in // PIECES, (p + 1) * n_in // PIECES, conv1_outer, 0)
-    reduce_stats(0, n_in, 0)
+        g = 2 * p // PIECES
+        body = conv1_outer(sa[g], g * half_in)
+        lax.fori_loop(p * n_in // PIECES, (p + 1) * n_in // PIECES, body, 0)
+        if 2 * (p + 1) % PIECES == 0:
+            start(g)
+
+    relay(0)
+    relay(1)
+    finish(0, 0, half_in, 0, n_in)
 
     for p in range(PIECES):
 
@@ -304,7 +325,7 @@
         def _():
             down1(p).wait_send()
 
-    def norm_to(src, dst, count):
+    def norm_to(src, dst, j0, j1):
         def body(j, carry):
             lanes = lanes_of(j)
             for k in range(pixels // step):
@@ -312,9 +333,7 @@
                 dst[span, lanes] = normal(src[span, lanes], j)
             return carry
 
-        lax.fori_loop(0, count, body, 0)
-
-    norm_to(first, act1, n_in)
+        lax.fori_loop(j0, j1, body, 0)
 
     def up2(n):
         return pltpu.make_async_remote_copy(
@@ -336,20 +355,33 @@
             device_id_type=MESH,
         )
 
-    def project(act, w_ref, dst, buf, count, after):
+    per = NCOL // LANES
+
+    def project_first(act, w_ref, dst, k1):
         def body(n, carry):
             wide = pl.ds(pl.multiple_of(n * NCOL, NCOL), NCOL)
-            y = jnp.dot(act[...], w_ref[:, wide], preferred_element_type=F32)
+            dst[:, wide] = jnp.dot(act[:, :k1], w_ref[:k1, wide], preferred_element_type=F32)
+            return carry
+
+        lax.fori_loop(0, dst.shape[1] // NCOL, body, 0)
+
+    def project_rest(act, w_ref, dst, k0, n0, n1, buf, after):
+        count = (n1 - n0) * per
+
+        def body(n, carry):
+            wide = pl.ds(pl.multiple_of(n * NCOL, NCOL), NCOL)
+            y = jnp.dot(act[:, k0:], w_ref[k0:, wide], preferred_element_type=F32)
+            y = y + dst[:, wide]
             dst[:, wide] = y
             s1 = fold(y)
             s2 = fold(y * y)
-            for q in range(NCOL // LANES):
+            for q in range(per):
                 part = slice(q * LANES, (q + 1) * LANES)
-                put_stats(buf, sp, n * (NCOL // LANES) + q, count, s1[:, part], s2[:, part])
+                put_stats(buf, sp, (n - n0) * per + q, count, s1[:, part], s2[:, part])
             after(n, y)
             return carry
 
-        lax.fori_loop(0, count * LANES // NCOL, body, 0)
+        lax.fori_loop(n0, n1, body, 0)
 
     n_wide = c_mid // NCOL
     early = n_wide // 2
@@ -380,9 +412,19 @@
 
         lax.fori_loop(early, n_wide, body, 0)
 
+    half_mid = n_mid // 2
+    norm_to(first, act1, 0, half_in)
     load_w1.wait()
-    project(act1, w1_ref, second, sa1, n_mid, send_edges)
-    reduce_stats(1, n_mid, 2 * n_in, send_late)
+    project_first(act1, w1_ref, second, half_in * LANES)
+    finish(1, half_in, half_in, 0, n_in)
+    norm_to(first, act1, half_in, n_in)
+    project_rest(act1, w1_ref, second, half_in * LANES, 0, early, sa2, send_edges)
+    start(2)
+    project_rest(act1, w1_ref, second, half_in * LANES, early, n_wide, sa3, send_edges)
+    start(3)
+    send_late()
+    relay(2)
+    relay(3)
 
     def wait_edges(n, carry):
         @pl.when(has_top)
@@ -403,9 +445,8 @@
     def _():
         halo2[1] = jnp.zeros(halo2.shape[1:], BF16)
 
-    lax.fori_loop(0, n_wide, wait_edges, 0)
-
-    def conv2(n, carry):
+
+    def conv2(buf, n0, n, carry):
         for q in range(NCOL // LANES):
             j = n * (NCOL // LANES) + q
             lanes = lanes_of(j)
@@ -421,16 +462,32 @@
                 xp[j, r, PAD : PAD + cols, :] = top[r * cols : (r + 1) * cols]
                 xp[j, rows + RATE + r, PAD : PAD + cols, :] = bot[r * cols : (r + 1) * cols]
             s1, s2 = conv_rows(j, list(range(rows)), d2_ref, second, zero8, zero8)
-            put_stats(sa2, sp, j, n_mid, s1, s2)
+            put_stats(buf, sp, j - n0 * per, half_mid, s1, s2)
         return carry
 
-    lax.fori_loop(0, n_wide, conv2, 0)
-    reduce_stats(2, n_mid, 2 * n_in + 2 * n_mid)
-    norm_to(second, act3, n_mid)
-
+    at2, at3 = 2 * n_in, 2 * n_in + 2 * n_mid
+    finish(2, 0, half_mid, at2, n_mid)
+    lax.fori_loop(0, early, wait_edges, 0)
+    lax.fori_loop(0, early, functools.partial(conv2, sa4, 0), 0)
+    start(4)
+    finish(3, half_mid, half_mid, at2, n_mid)
+    lax.fori_loop(early, n_wide, wait_edges, 0)
+    lax.fori_loop(early, n_wide - 1, functools.partial(conv2, sa5, early), 0)
+    relay(4)
+    lax.fori_loop(n_wide - 1, n_wide, functools.partial(conv2, sa5, early), 0)
+    start(5)
+    finish(4, 0, half_mid, at3, n_mid)
+    relay(5)
+
+    norm_to(second, act3, 0, half_mid)
     load_w2.wait()
-    project(act3, w2_ref, fourth, sa3, n_out, lambda n, y: None)
-    reduce_stats(3, n_out, 2 * n_in + 4 * n_mid)
+    project_first(act3, w2_ref, fourth, half_mid * LANES)
+    finish(5, half_mid, half_mid, at3, n_mid)
+    norm_to(second, act3, half_mid, n_mid)
+    project_rest(act3, w2_ref, fourth, half_mid * LANES, 0, c_out // NCOL, sa6, lambda n, y: None)
+    start(6)
+    relay(6)
+    finish(6, 0, n_out, 2 * n_in + 4 * n_mid, n_out)
 
     for q, ref in enumerate((mean_out, fac_out, shift_out)):
         for j in range(n_out):
@@ -476,7 +533,7 @@
     n_in, n_mid, n_out = c_in // LANES, c_mid // LANES, c_out // LANES
     any_spec = pl.BlockSpec(memory_space=pl.ANY)
     vmem = pl.BlockSpec(memory_space=pltpu.VMEM)
-    counts = (n_in, n_mid, n_mid, n_out)
+    counts = (n_in // 2,) * 2 + (n_mid // 2,) * 4 + (n_out,)
     edge = RATE * cols
     n_wide = c_mid // NCOL
     coef_rows = max(n_out, 8 * n_in)
@@ -514,10 +571,10 @@
             DMA((2, PIECES)),
             DMA((2, n_wide)),
             DMA((2, n_wide)),
-            DMA((4, n_space - 1)),
-            DMA((4, n_space - 1)),
-            DMA((4, n_batch - 1)),
-            DMA((4, n_batch - 1)),
+            DMA((7, n_space - 1)),
+            DMA((7, n_space - 1)),
+            DMA((7, n_batch - 1)),
+            DMA((7, n_batch - 1)),
         ],
         compiler_params=pltpu.CompilerParams(
             collective_id=0, has_side_effects=True, vmem_limit_bytes=56 * 1024 * 1024

time: 64.9 us -> 63.2 us (0.974)
  Pallas kernels: 60.9 us -> 59.3 us
    pallas_call x1, Pallas kernels: 60.9 us -> 59.3 us  [per_device(): pl.pallas_call(functools.partial(kernel, n_space, n_batch), out_shape=(pl...]
where the time goes in v2:
time: 63.2 us; the launch traced here: 63 us
  Pallas kernels  59.3 us (94%)
  other arithmetic  3.68 us (6%)
    pallas_call x1, Pallas kernels, per_device(): pl.pallas_call(functools.partial(kernel, n_space, n_batch), out_shape=(pl...  59.3 us
    convert_element_type x1, other arithmetic, per_device(): out = jnp.maximum((fourth - mean) * fac + shift, 0.0).astype(BF16)  3.68 us

profile of v2, /device:TPU:0, one launch (start us, length us, event | category | flops | bytes accessed | tf_op | source)
XLA Modules:
  0.0 63.0 jit_solution(8779906596796335690)
XLA Ops:
  0.0 59.3 %exit_block.1 = (f32[864,2048]{1,0:T(8,128)S(1)}, f32[1,2048]{1,0:T(1,128)}, f32[1,2048]{1,0:T(1,128)}, f32[1,2048]{1,0:T(1,128)}) custom-call(bf16[12,72,1024]{2,1,0:T(8,128)(2,1)} %bitcast.5, bf16[1024,1536]{1,0:T(8,128)(2,1)} %w1_hbm.1, bf16[1536,2048]{1,0:T(8,128)(2,1)} %w2_hbm.1, bf16[3,3,1024]{2,1,0:T(4,128)(2,1)} %d1_ref.1, ...), custom_call_target="tpu_custom_call" | custom-call | tf_op jit(solution)/shard_map/exit_block/pallas_call | solution.py:541
  59.3 3.7 %maximum_convert_fusion = bf16[864,2048]{1,0:T(8,128)(2,1)} fusion(f32[864,2048]{1,0:T(8,128)S(1)} %get-tuple-element.9, f32[2048]{0:T(1024)} %bitcast.8, f32[2048]{0:T(1024)} %bitcast.7, f32[2048]{0:T(1024)} %bitcast.6), kind=kLoop, calls=%fused_computation | loop fusion | flops 8847360 | bytes 10641408 | tf_op jit(solution)/shard_map/convert_element_type | solution.py:603
